TPU v7x, 32 devices: a whole 2x2x4 slice. The times are simulated.
32 devices in a mesh: row: 4 (over y, core), col: 8 (over z, x).
Axes of the slice: x: 2, y: 2, z: 4, core: 2. Of those that a mesh axis runs over, the one named last changes fastest.
Arguments:
- text_features: bfloat16 [5, 1024, 3584], P(None, ('row', 'col')), may hold values from -18 to 18
- vision_features: bfloat16 [6, 1024, 1024], P(None, ('row', 'col')), may hold values from -18 to 18
Outputs:
- stimulus_terms: float32 [1024, 30], P(('row', 'col'))
- cka: float32 [5, 6], replicated
All inputs are finite; a program needn't handle non-finite values.
Results may differ from a plain program's by a relative error of at most 0.0003.
Values may be sent and summed in bfloat16 or wider, within the bound.
No kernel may reach another device: no remote copies, remote signals or barrier semaphores. Data moves between devices by JAX's collectives and lax.ppermute only.
A program may use at most 192 MiB of HBM per device.

v0:
```python
import jax
import jax.numpy as jnp
from jax import lax
from jax.sharding import PartitionSpec as P


def center_with(features, totals, stimuli_count):
    values = features.astype(jnp.float32)
    return (values - totals[:, None, :] / stimuli_count).astype(jnp.bfloat16)


def local(text_features, vision_features):
    text_layers = text_features.shape[0]
    vision_layers = vision_features.shape[0]
    stimuli_count = text_features.shape[1] * lax.axis_size("row") * lax.axis_size("col")
    text_block, vision_block = (
        lax.all_gather(text_features, "col", axis=1, tiled=True),
        lax.all_gather(vision_features, "col", axis=1, tiled=True),
    )
    text_set, vision_set = (
        lax.all_gather(text_features, "row", axis=1, tiled=True),
        lax.all_gather(vision_features, "row", axis=1, tiled=True),
    )
    text_total, vision_total = lax.psum(
        (
            jnp.sum(text_block.astype(jnp.float32), axis=1),
            jnp.sum(vision_block.astype(jnp.float32), axis=1),
        ),
        "row",
    )
    text_block = center_with(text_block, text_total, stimuli_count)
    text_set = center_with(text_set, text_total, stimuli_count)
    vision_block = center_with(vision_block, vision_total, stimuli_count)
    vision_set = center_with(vision_set, vision_total, stimuli_count)
    text_tiles = jnp.einsum(
        "lrd,lcd->lrc", text_block, text_set, preferred_element_type=jnp.float32
    )
    vision_tiles = jnp.einsum(
        "lrd,lcd->lrc", vision_block, vision_set, preferred_element_type=jnp.float32
    )
    row_share = jnp.einsum(
        "arc,brc->rab", text_tiles, vision_tiles, precision=lax.Precision.HIGHEST
    )
    block_rows = row_share.shape[0]
    cross_part = jnp.sum(row_share, axis=0)
    text_part = jnp.sum(text_tiles * text_tiles, axis=(1, 2))
    vision_part = jnp.sum(vision_tiles * vision_tiles, axis=(1, 2))
    cross, text_self, vision_self = lax.psum((cross_part, text_part, vision_part), ("row", "col"))
    own_share = lax.psum_scatter(
        row_share.reshape(block_rows, text_layers * vision_layers),
        "col",
        scatter_dimension=0,
        tiled=True,
    )
    scale = 1.0 / jnp.sqrt(text_self[:, None] * vision_self[None, :])
    stimulus_terms = own_share * (scale.reshape(1, text_layers * vision_layers) * stimuli_count)
    return (stimulus_terms, cross * scale)


def solution(mesh):
    in_specs = (P(None, ("row", "col"), None), P(None, ("row", "col"), None))
    out_specs = (P(("row", "col"), None), P())
    return jax.shard_map(local, mesh=mesh, in_specs=in_specs, out_specs=out_specs, check_vma=False)
```

profile of v0, /device:TPU:0, one launch (start us, length us, event | category | flops | bytes accessed | tf_op | source)
XLA Modules:
  0.0 381.2 jit_solution(2243413906863889780)
XLA Ops:
  7.2 0.0 all-gather.5.cloned.1.call-start
  7.2 0.7 all-gather.5.cloned.1.call-update
  7.9 0.0 all-gather.9.cloned.1.call-start
  7.9 0.7 all-gather.9.cloned.1.call-update
  8.6 0.0 all-gather.11.cloned.1.call-start
  8.7 0.7 all-gather.11.cloned.1.call-update
  9.4 0.0 all-reduce.3.cloned.1.call-start
  9.4 137.5 %all-gather.5.cloned.1.call-done = bf16[5,256,3584]{2,1,0:T(8,128)(2,1)} async-done(((bf16[5,32,3584]{2,1,0:T(8,128)(2,1)}), bf16[5,256,3584]{2,1,0:T(8,128)(2,1)}) %all-gather.5.cloned.1.call-update) | async-done | bytes 9175056 | tf_op jit(solution)/shard_map/all_gather | solution.py:17
  147.0 5.5 %convert_reduce_fusion = f32[5,3584]{1,0:T(8,128)} fusion(bf16[5,256,3584]{2,1,0:T(8,128)(2,1)} %all-gather.5.cloned.1.call-done), kind=kLoop, calls=%fused_computation.1 | loop fusion | flops 9157120 | bytes 9246720 | tf_op jit(solution)/shard_map/reduce_sum | solution.py:26
  152.5 0.0 all-reduce.3.cloned.1.call-update
  152.5 0.0 all-gather.7.cloned.1.call-start
  152.6 0.5 all-gather.7.cloned.1.call-update
  153.1 0.0 reduce-scatter.4.cloned.1.call-start
  153.2 54.2 %all-gather.9.cloned.1.call-done = bf16[6,256,1024]{2,1,0:T(8,128)(2,1)} async-done(((bf16[6,32,1024]{2,1,0:T(8,128)(2,1)}), bf16[6,256,1024]{2,1,0:T(8,128)(2,1)}) %all-gather.9.cloned.1.call-update) | async-done | bytes 3145744 | tf_op jit(solution)/shard_map/all_gather | solution.py:18
  207.4 2.5 convert_reduce_fusion.1
  209.9 11.1 %psum.36 = f32[6,1024]{1,0:T(8,128)S(1)} all-reduce(f32[6,1024]{1,0:T(8,128)S(1)} %convert_reduce_fusion.1), channel_id=1, replica_groups=mesh['row'=4,'col'=8] {'row'}, use_global_device_ids=true, to_apply=%region_3.0 | all-reduce | flops 6144 | bytes 49152 | tf_op jit(solution)/shard_map/psum | solution.py:24
  221.0 6.5 %all-gather.11.cloned.1.call-done = bf16[6,128,1024]{2,1,0:T(8,128)(2,1)} async-done(((bf16[6,32,1024]{2,1,0:T(8,128)(2,1)}), bf16[6,128,1024]{2,1,0:T(8,128)(2,1)}) %all-gather.11.cloned.1.call-update) | async-done | bytes 1572880 | tf_op jit(solution)/shard_map/all_gather | solution.py:22
  227.5 3.5 multiply_reduce_fusion
  231.0 28.9 %all-reduce.3.cloned.1.call-done = f32[5,3584]{1,0:T(8,128)} async-done(((f32[5,3584]{1,0:T(8,128)}), f32[5,3584]{1,0:T(8,128)}) %all-reduce.3.cloned.1.call-update) | async-done | bytes 71696 | tf_op jit(solution)/shard_map/psum | solution.py:24
  259.9 0.9 broadcast_multiply_fusion
  260.8 38.6 %all-gather.7.cloned.1.call-done = bf16[5,128,3584]{2,1,0:T(8,128)(2,1)} async-done(((bf16[5,32,3584]{2,1,0:T(8,128)(2,1)}), bf16[5,128,3584]{2,1,0:T(8,128)(2,1)}) %all-gather.7.cloned.1.call-update) | async-done | bytes 4587536 | tf_op jit(solution)/shard_map/all_gather | solution.py:21
  299.4 7.6 %multiply_reduce_fusion.1 = (f32[5]{0:T(128)S(1)}, f32[5,256,128]{2,1,0:T(8,128)S(1)}) fusion(bf16[5,128,3584]{2,1,0:T(8,128)(2,1)} %all-gather.7.cloned.1.call-done, f32[5,3584]{1,0:T(8,128)S(1)} %broadcast_multiply_fusion, bf16[5,256,3584]{2,1,0:T(8,128)(2,1)} %all-gather.5.cloned.1.call-done), kind=kOutput, calls=%fused_computation.18 | convolution fusion | flops 1195376640 | bytes 14489620 | tf_op jit(solution)/shard_map/lrd,lcd->lrc/dot_general | solution.py:35
  307.0 2.6 fusion.15
  309.6 0.8 reshape.34
  310.4 0.0 reduce-scatter.4.cloned.1.call-update
  310.5 39.5 %all-reduce = (f32[6]{0:T(128)S(1)}, f32[5]{0:T(128)S(1)}, f32[5,6]{1,0:T(8,128)S(1)}) all-reduce(f32[6]{0:T(128)S(1)} %get-tuple-element.11, f32[5]{0:T(128)S(1)} %get-tuple-element.13, f32[5,6]{1,0:T(8,128)S(1)} %get-tuple-element.15), channel_id=1, replica_groups=mesh['row'=4,'col'=8] {'row','col'}, use_global_device_ids=true, to_apply=%region_8.0 | all-reduce | flops 41 | bytes 328 | tf_op jit(solution)/shard_map/psum | solution.py:48
  349.9 0.7 fusion.13
  350.6 0.1 mul.53
  350.7 22.1 %reduce-scatter.4.cloned.1.call-done = f32[32,30]{1,0:T(8,128)} async-done(((f32[256,30]{1,0:T(8,128)}), f32[32,30]{1,0:T(8,128)}) %reduce-scatter.4.cloned.1.call-update) | async-done | bytes 3856
  372.8 0.8 copy.15
  373.6 0.1 broadcast_multiply_fusion.2
  373.7 0.7 copy.13
  (1 shorter events, 0.0 us)
Async XLA Ops:
  7.2 139.8 %all-gather.5.cloned.1.call-start = ((), (), s32[]{:S(2)}) async-start(), calls=%async_computation.1 | async-start | bytes 10321920 | tf_op jit(solution)/shard_map/all_gather | solution.py:17
  7.9 199.5 %all-gather.9.cloned.1.call-start = ((), (), s32[]{:S(2)}) async-start(), calls=%async_computation.4 | async-start | bytes 3538944 | tf_op jit(solution)/shard_map/all_gather | solution.py:18
  8.6 218.9 %all-gather.11.cloned.1.call-start = ((), (), s32[]{:S(2)}) async-start(), calls=%async_computation.5 | async-start | bytes 1966080 | tf_op jit(solution)/shard_map/all_gather | solution.py:22
  9.4 250.6 %all-reduce.3.cloned.1.call-start = ((), (), s32[]{:S(2)}) async-start(), calls=%async_computation.2 | async-start | bytes 229376 | tf_op jit(solution)/shard_map/psum | solution.py:24
  152.5 146.9 %all-gather.7.cloned.1.call-start = ((), (), s32[]{:S(2)}) async-start(), calls=%async_computation.3 | async-start | bytes 5734400 | tf_op jit(solution)/shard_map/all_gather | solution.py:21
  153.1 219.7 %reduce-scatter.4.cloned.1.call-start = ((), (), s32[]{:S(2)}) async-start(), calls=%async_computation.6 | async-start | bytes 147456
Sparse Core Ops, SparseCore 0:
  10.2 136.7 all-gather.4
  149.1 58.1 all-gather.8
  208.9 18.5 all-gather.10
  229.7 30.1 all-reduce.2
  261.3 38.0 all-gather.6
  310.6 62.1 reduce-scatter.3
where the time goes:
time: 382 us; the launch traced here: 381 us
  waiting for transfers between devices  291 us (76%)
  blocking collectives  50.6 us (13%)
  between operations  14.1 us (4%)
  matrix products  13.6 us (4%)
  other arithmetic  9.69 us (3%)
    all_gather x1, waiting for transfers between devices, local(): lax.all_gather(text_features, 'col', axis=1, tiled=True)  138 us
    all_gather x1, waiting for transfers between devices, local(): lax.all_gather(vision_features, 'col', axis=1, tiled=True)  54.2 us
    psum x1, blocking collectives, local(): lax.psum((cross_part, text_part, vision_part), ('row', 'col'))  39.5 us
    all_gather x1, waiting for transfers between devices, local(): lax.all_gather(text_features, 'row', axis=1, tiled=True)  38.6 us
    psum x1, waiting for transfers between devices, local(): lax.psum((jnp.sum(text_block.astype(jnp.float32), axis=1), jnp.sum(vision...  28.9 us
    unnamed x7, waiting for transfers between devices  24.8 us
    psum x1, blocking collectives, local(): lax.psum((jnp.sum(text_block.astype(jnp.float32), axis=1), jnp.sum(vision...  11.1 us
  transfers between devices with their start and end apart: 6, of which 6 were waited for; matrix products, arithmetic and copies ran while one was open for 3% of the time, Pallas kernels for 0%

commit v1 on v0

v1 whole, which is shorter than its diff:
```python
import math

import jax
import jax.numpy as jnp
import numpy as np
from jax import lax
from jax.experimental import pallas as pl
from jax.experimental.pallas import tpu as pltpu
from jax.sharding import PartitionSpec as P


AXES = ("row", "col")
NT = (((1,), (1,)), ((), ()))


class Grid:
    def __init__(self, mesh):
        devices = mesh.devices
        rows, cols = devices.shape
        flat = list(devices.flat)
        places = [getattr(d, "coords", None) for d in flat]
        if all(p is not None for p in places):
            at = [(*p[:3], getattr(d, "core_on_chip", 0)) for p, d in zip(places, flat)]
        else:
            at = [(0, r, c, 0) for r in range(rows) for c in range(cols)]
        levels = [sorted({a[k] for a in at}) for k in range(4)]
        self.at = [tuple(levels[k].index(a[k]) for k in range(4)) for a in at]
        self.size = tuple(len(v) for v in levels)
        self.index = {a: i for i, a in enumerate(self.at)}
        if len(self.index) != len(flat) or len(flat) != math.prod(self.size):
            self.at = [(0, r, c, 0) for r in range(rows) for c in range(cols)]
            self.size = (1, rows, cols, 1)
            self.index = {a: i for i, a in enumerate(self.at)}

    def moved(self, i, shift):
        return self.index[tuple((p + s) % n for p, s, n in zip(self.at[i], shift, self.size))]

    def pairs(self, shift, senders=None):
        return [(i, self.moved(i, shift)) for i in range(len(self.at)) if senders is None or senders(self.at[i])]


def pack_kernel(kt, kv, width, start, text_ref, vision_ref, packed_ref, sums_ref):
    for k in range(kt * text_ref.shape[0], start):
        packed_ref[k] = jnp.zeros(packed_ref.shape[1:], packed_ref.dtype)
        sums_ref[pl.ds(k, 1), :] = jnp.zeros((1, width), jnp.float32)
    for ref, per, first in ((text_ref, kt, 0), (vision_ref, kv, start)):
        for layer in range(ref.shape[0]):
            for k in range(per):
                values = ref[layer, :, k * width : (k + 1) * width]
                packed_ref[first + layer * per + k] = values
                sums_ref[pl.ds(first + layer * per + k, 1), :] = jnp.sum(
                    values.astype(jnp.float32), axis=0, keepdims=True
                )


def pack(text, vision, kt, kv, width, start):
    chunks = start + kv * vision.shape[0]
    rows = text.shape[1]
    return pl.pallas_call(
        lambda *refs: pack_kernel(kt, kv, width, start, *refs),
        out_shape=(
            jax.ShapeDtypeStruct((chunks, rows, width), text.dtype),
            jax.ShapeDtypeStruct((chunks, width), jnp.float32),
        ),
        name="pack",
    )(text, vision)


def tiles_kernel(
    la, lb, kt, kv, rows, na, nb, ndest, count,
    dest_ref, weight_ref, *refs,
):
    ins, payload_ref, scratch = refs[: 2 * (na + nb) + 2], refs[2 * (na + nb) + 2], refs[2 * (na + nb) + 3 :]
    ac, bc, k1, k2, g1, g2, cols_ref, rows_ref = scratch
    step = pl.program_id(0)
    width = ins[0].shape[-1]

    def layer(blocks, mean_ref, per, out1, out2, i):
        for k in range(per):
            mean = mean_ref[0, k : k + 1, :] * (1.0 / count)
            for j, ref in enumerate(blocks):
                centered = (ref[k].astype(jnp.float32) - mean).astype(jnp.bfloat16)
                if j < na:
                    ac[pl.ds(j * rows, rows), pl.ds(k * width, width)] = centered
                if j == 0:
                    bc[pl.ds(nb * rows, rows), pl.ds(k * width, width)] = centered
                if j >= na:
                    bc[pl.ds((j - na) * rows, rows), pl.ds(k * width, width)] = centered
        a = ac[:, pl.ds(0, per * width)]
        b = bc[:, pl.ds(0, per * width)]
        out1[i] = lax.dot_general(a, b, NT, preferred_element_type=jnp.float32)
        out2[i] = lax.dot_general(b[: nb * rows], a, NT, preferred_element_type=jnp.float32)

    @pl.when(step < la)
    def _():
        layer(ins[: na + nb], ins[-2], kt, k1, k2, step)

    @pl.when(step < lb)
    def _():
        layer(ins[na + nb : 2 * (na + nb)], ins[-1], kv, g1, g2, step)

    @pl.when(step == max(la, lb) - 1)
    def _():
        pairs = la * lb
        nbr = (nb + 1) * rows
        cols_ref[...] = jnp.zeros_like(cols_ref)
        rows_ref[...] = jnp.zeros_like(rows_ref)
        lane = lax.broadcasted_iota(jnp.int32, (1, 128), 1)
        wlast = weight_ref[0]
        block = lane // rows
        cell = jnp.where(block < nb - 1, 2.0, jnp.where(block == nb - 1, 2.0 * wlast, 1.0))
        cell = jnp.where(block <= nb, cell, 0.0)
        for a in range(la):
            for b in range(lb):
                p = a * lb + b
                cols_ref[p : p + 1, 0:nbr] = jnp.sum(k1[a] * g1[b], axis=0, keepdims=True)
                prod = k2[a] * g2[b]
                rows_ref[p : p + 1, :] = jnp.sum(prod[: (nb - 1) * rows], axis=0, keepdims=True) + wlast * jnp.sum(
                    prod[(nb - 1) * rows :], axis=0, keepdims=True
                )
        for a in range(la):
            cols_ref[pairs + a : pairs + a + 1, 0:nbr] = jnp.sum(k1[a] * k1[a], axis=0, keepdims=True)
        for b in range(lb):
            cols_ref[pairs + la + b : pairs + la + b + 1, 0:nbr] = jnp.sum(g1[b] * g1[b], axis=0, keepdims=True)
        totals = jnp.sum((cols_ref[...] * cell).T, axis=0, keepdims=True)
        q_count = 128 // rows
        sub = lax.broadcasted_iota(jnp.int32, (8, 128), 0)
        lane8 = lax.broadcasted_iota(jnp.int32, (8, 128), 1)
        spot = (lane8 // rows) * 8 + sub
        own = lane8 % rows
        spread = jnp.broadcast_to(totals, (8, 128))

        def shifted(x, by):
            by %= 128
            return pltpu.roll(x, by, 1) if by else x

        base = jnp.zeros((8, 128), jnp.float32)
        q_cross, q_self = pairs // 8, (pairs + 1) // 8
        base = jnp.where((spot == pairs) & (own < pairs), shifted(spread, q_cross * rows), base)
        base = jnp.where((spot == pairs + 1) & (own < la + lb), shifted(spread, q_self * rows - pairs), base)
        for d in range(ndest):
            payload_ref[d] = base
        for j in range(na + nb):
            tile = base
            for q in range(q_count):
                if j < na:
                    c0 = j * rows
                    part = shifted(rows_ref[8 * q : 8 * q + 8, c0 // 128 * 128 : c0 // 128 * 128 + 128], q * rows - c0 % 128)
                    if j == 0:
                        part = part + shifted(cols_ref[8 * q : 8 * q + 8, :], (q - nb) * rows)
                else:
                    part = shifted(cols_ref[8 * q : 8 * q + 8, :], (q - (j - na)) * rows)
                    if j == na + nb - 1:
                        part = part * wlast
                tile = jnp.where((lane8 // rows == q) & (spot < pairs), part, tile)
            payload_ref[dest_ref[j]] = tile


def tiles(a_blocks, b_blocks, totals, dest, weight, la, lb, kt, kv, start, count, ndest):
    na, nb = len(a_blocks), len(b_blocks)
    blocks = [*a_blocks, *b_blocks]
    rows, width = blocks[0].shape[1:]
    assert (nb + 1) * rows <= 128 and 128 % rows == 0
    assert 8 * (128 // rows) >= la * lb + 2 and la * lb + la + lb <= 128 and la * lb <= rows and nb >= 1
    steps = max(la, lb)
    smem = pl.BlockSpec(memory_space=pltpu.SMEM)
    text_spec = pl.BlockSpec((kt, rows, width), lambda i: (jnp.minimum(i, la - 1), 0, 0))
    vision_spec = pl.BlockSpec((kv, rows, width), lambda i: (start // kv + jnp.minimum(i, lb - 1), 0, 0))
    mean_t = totals[: la * kt].reshape(la, kt, width)
    mean_v = totals[start:].reshape(lb, kv, width)
    return pl.pallas_call(
        lambda *refs: tiles_kernel(la, lb, kt, kv, rows, na, nb, ndest, count, *refs),
        grid=(steps,),
        in_specs=[smem, smem]
        + [text_spec] * (na + nb)
        + [vision_spec] * (na + nb)
        + [
            pl.BlockSpec((1, kt, width), lambda i: (jnp.minimum(i, la - 1), 0, 0)),
            pl.BlockSpec((1, kv, width), lambda i: (jnp.minimum(i, lb - 1), 0, 0)),
        ],
        out_specs=pl.BlockSpec((ndest, 8, 128), lambda i: (0, 0, 0)),
        out_shape=jax.ShapeDtypeStruct((ndest, 8, 128), jnp.float32),
        scratch_shapes=[
            pltpu.VMEM((na * rows, max(kt, kv) * width), jnp.bfloat16),
            pltpu.VMEM(((nb + 1) * rows, max(kt, kv) * width), jnp.bfloat16),
            pltpu.VMEM((la, na * rows, (nb + 1) * rows), jnp.float32),
            pltpu.VMEM((la, nb * rows, na * rows), jnp.float32),
            pltpu.VMEM((lb, na * rows, (nb + 1) * rows), jnp.float32),
            pltpu.VMEM((lb, nb * rows, na * rows), jnp.float32),
            pltpu.VMEM((128, 128), jnp.float32),
            pltpu.VMEM((8 * (128 // rows), max(128, na * rows)), jnp.float32),
        ],
        compiler_params=pltpu.CompilerParams(vmem_limit_bytes=56 * 1024 * 1024),
        name="tiles",
    )(dest, weight, *blocks, *blocks, mean_t, mean_v)


def finish_kernel(la, lb, rows, count, in_ref, terms_ref, cka_ref):
    pairs = la * lb
    total = jnp.sum(in_ref[...], axis=0)
    spots = jnp.concatenate([total[:, q * rows : (q + 1) * rows] for q in range(128 // rows)], axis=0)
    cross = spots[pairs : pairs + 1, :]
    selves = jnp.broadcast_to(spots[pairs + 1 : pairs + 2, :], (rows, rows)).T
    sub = lax.broadcasted_iota(jnp.int32, (rows, rows), 0)
    lane = lax.broadcasted_iota(jnp.int32, (rows, rows), 1)
    text = jnp.sum(jnp.where(sub == lane // lb, selves, 0.0), axis=0, keepdims=True)
    vision = jnp.sum(jnp.where(sub == la + lane % lb, selves, 0.0), axis=0, keepdims=True)
    inside = lax.broadcasted_iota(jnp.int32, (1, rows), 1) < pairs
    scale = 1.0 / jnp.sqrt(jnp.where(inside, text * vision, 1.0))
    terms = spots.T * (scale * count) if spots.shape[0] == rows else spots.T[:, :rows] * (scale * count)
    terms_ref[...] = terms[:, :pairs]
    cka = cross * scale
    for a in range(la):
        cka_ref[a : a + 1, :] = cka[:, a * lb : (a + 1) * lb]


def finish(received, la, lb, rows, count):
    return pl.pallas_call(
        lambda *refs: finish_kernel(la, lb, rows, count, *refs),
        out_shape=(
            jax.ShapeDtypeStruct((rows, la * lb), jnp.float32),
            jax.ShapeDtypeStruct((la, lb), jnp.float32),
        ),
        name="finish",
    )(received)


def solution(mesh):
    grid = Grid(mesh)
    nx, ny, nz, nc = grid.size
    ndev = len(grid.at)

    def send(value, shift, senders=None):
        return lax.ppermute(value, AXES, grid.pairs(shift, senders))

    def half_sender(place):
        z = place[2]
        return (z < nz // 2) == ((z % (nz // 2)) % 2 == 0)

    def body(text, vision):
        la, rows, da = text.shape
        lb, _, db = vision.shape
        count = rows * ndev
        width = math.gcd(da, db)
        kt, kv = da // width, db // width
        start = -(-la * kt // kv) * kv
        me = lax.axis_index(AXES)
        own, sums = pack(text, vision, kt, kv, width, start)
        chunks = own.shape[0]

        b_blocks, b_shifts = [], []
        full_shifts = range(1, (nz + 1) // 2)
        for d in full_shifts:
            b_blocks.append(send(own, (0, 0, d, 0)))
            b_shifts.append((0, 0, d, 0))

        for d in range(1, nc):
            sums = sums + send(sums, (0, 0, 0, d))
        part = sums
        for d in range(1, nx):
            sums = sums + send(part, (d, 0, 0, 0))
        part = sums
        for d in range(1, ny):
            sums = sums + send(part, (0, d, 0, 0))
        part = sums
        for d in range(1, nz):
            sums = sums + send(part, (0, 0, d, 0))

        plane = {(0, 0): own}
        for d in range(1, nx):
            plane[d, 0] = send(own, (d, 0, 0, 0))
        for d in range(1, ny):
            plane[0, d] = send(own, (0, d, 0, 0))
        half = chunks // 2
        for dx in range(1, nx):
            for dy in range(1, ny):
                first = send(plane[dx, 0][:half], (0, dy, 0, 0))
                second = send(plane[0, dy][half:], (dx, 0, 0, 0))
                plane[dx, dy] = jnp.concatenate([first, second], axis=0)
        a_blocks, a_shifts = [], []
        for (dx, dy), block in plane.items():
            a_blocks.append(block)
            a_shifts.append((dx, dy, 0, 0))
            for dc in range(1, nc):
                a_blocks.append(send(block, (0, 0, 0, dc)))
                a_shifts.append((dx, dy, 0, dc))

        weight = np.zeros((ndev,), np.float32)
        if nz % 2 == 0:
            b_blocks.append(send(own, (0, 0, nz // 2, 0), half_sender))
            b_shifts.append((0, 0, nz // 2, 0))
            for i in range(ndev):
                if half_sender(grid.at[i]):
                    weight[grid.moved(i, (0, 0, nz // 2, 0))] = 1.0
        else:
            weight[:] = 1.0
        shifts = a_shifts + b_shifts
        table = np.array(
            [[grid.moved(i, tuple(-s for s in shift)) for shift in shifts] for i in range(ndev)], np.int32
        )
        dest = lax.dynamic_index_in_dim(jnp.asarray(table), me, 0, keepdims=False)
        w = lax.dynamic_slice_in_dim(jnp.asarray(weight), me, 1)
        payload = tiles(a_blocks, b_blocks, sums, dest, w, la, lb, kt, kv, start, count, ndev)
        received = lax.all_to_all(payload, AXES, 0, 0, tiled=True)
        return finish(received, la, lb, rows, count)

    spec = P(None, AXES, None)
    return jax.shard_map(body, mesh=mesh, in_specs=(spec, spec), out_specs=(P(AXES, None), P()), check_vma=False)
```

time: 382 us -> 143 us (0.37)
  waiting for transfers between devices: 291 us -> 85.8 us
  blocking collectives: 50.6 us -> 11.1 us
  starting transfers between devices: 0.23 us -> 22.3 us
  Pallas kernels: 0 us -> 17.9 us
  matrix products: 13.6 us -> 0 us
  between operations: 14.1 us -> 0.71 us
  other arithmetic: 9.69 us -> 0.07 us
    all_gather x4 -> x0, waiting for transfers between devices: 237 us -> none  [the longest x1 138 us: local(): lax.all_gather(text_features, 'col', axis=1, tiled=True)]
    ppermute x0 -> x16, waiting for transfers between devices: none -> 85.8 us  [send(): return lax.ppermute(value, AXES, grid.pairs(shift, senders))]
    psum x2 -> x0, blocking collectives: 50.6 us -> none  [the longest x1 39.5 us: local(): lax.psum((cross_part, text_part, vision_part), ('row', 'col'))]
    psum x1 -> x0, waiting for transfers between devices: 28.9 us -> none  [local(): lax.psum((jnp.sum(text_block.astype(jnp.float32), axis=1), jnp.sum(vision...]
    unnamed x7 -> x0, waiting for transfers between devices: 24.8 us -> none
    ppermute x0 -> x16, starting transfers between devices: none -> 22.3 us  [send(): return lax.ppermute(value, AXES, grid.pairs(shift, senders))]
    pallas_call x0 -> x3, Pallas kernels: none -> 17.9 us  [the longest x1 13.2 us: tiles(): pl.pallas_call(lambda *refs: tiles_kernel(la, lb, kt, kv, rows, na, nb, n...]
    dot_general x3 -> x0, matrix products: 13.6 us -> none  [the longest x1 7.61 us: local(): jnp.einsum('lrd,lcd->lrc', text_block, text_set, preferred_element_type=j...]
  transfers between devices with their start and end apart: 6 -> 16, of which waited for: 6 -> 8; matrix products, arithmetic and copies ran while one was open for 3% -> 4% of each run, Pallas kernels for 0% -> 0%
where the time goes in v1:
time: 143 us
  waiting for transfers between devices  85.8 us (60%)
  starting transfers between devices  22.3 us (16%)
  Pallas kernels  17.9 us (13%)
  blocking collectives  11.1 us (8%)
  local copies, waits for them, and re-layouts  5.16 us (4%)
    ppermute x16, waiting for transfers between devices, send(): return lax.ppermute(value, AXES, grid.pairs(shift, senders))  85.8 us
    ppermute x16, starting transfers between devices, send(): return lax.ppermute(value, AXES, grid.pairs(shift, senders))  22.3 us
    pallas_call x1, Pallas kernels, tiles(): pl.pallas_call(lambda *refs: tiles_kernel(la, lb, kt, kv, rows, na, nb, n...  13.2 us
    all_to_all x1, blocking collectives, body(): received = lax.all_to_all(payload, AXES, 0, 0, tiled=True)  11.1 us
    pallas_call x1, Pallas kernels, pack(): pl.pallas_call(lambda *refs: pack_kernel(kt, kv, width, start, *refs), ou...  2.89 us
  transfers between devices with their start and end apart: 16, of which 8 were waited for; matrix products, arithmetic and copies ran while one was open for 4% of the time, Pallas kernels for 0%

profile of v1, /device:TPU:0, one launch (start us, length us, event | category | flops | bytes accessed | tf_op | source)
XLA Modules:
  0.0 143.1 jit_solution(18234376732909645095)
XLA Ops:
  0.6 2.9 %pack.1 = (bf16[48,32,512]{2,1,0:T(8,128)(2,1)}, f32[48,512]{1,0:T(8,128)}) custom-call(bf16[5,32,3584]{2,1,0:T(8,128)(2,1)} %refs_0_.1, bf16[6,32,1024]{2,1,0:T(8,128)(2,1)} %refs_1_.1), custom_call_target="tpu_custom_call" | custom-call | tf_op jit(solution)/shard_map/pack/pallas_call | solution.py:59
  3.5 0.0 copy-start.2
  3.5 3.0 %collective-permute-start.1 = (bf16[48,32,512]{2,1,0:T(8,128)(2,1)}, bf16[48,32,512]{2,1,0:T(8,128)(2,1)S(1)}, u32[]{:S(2)}, u32[]{:S(2)}) collective-permute-start(bf16[48,32,512]{2,1,0:T(8,128)(2,1)} %get-tuple-element.4.refs_2_.refs_12_), channel_id=1, source_target_pairs={{0,1},{1,0},{2,3},{3,2},{4,5},{5,4},{6,7},{7,6},{8,9},{9,8},{10,11... | collective-permute-start | bytes 4718600 | tf_op jit(solution)/shard_map/ppermute | solution.py:234
  6.5 1.5 %collective-permute-start.3 = (bf16[48,32,512]{2,1,0:T(8,128)(2,1)}, bf16[48,32,512]{2,1,0:T(8,128)(2,1)S(1)}, u32[]{:S(2)}, u32[]{:S(2)}) collective-permute-start(bf16[48,32,512]{2,1,0:T(8,128)(2,1)} %get-tuple-element.4.refs_2_.refs_12_), channel_id=1, source_target_pairs={{0,16},{1,17},{2,18},{3,19},{4,20},{5,21},{6,22},{7,23},{8,24},{9,... | collective-permute-start | bytes 4718600 | tf_op jit(solution)/shard_map/ppermute | solution.py:234
  8.0 5.7 %collective-permute-start.9 = (bf16[48,32,512]{2,1,0:T(8,128)(2,1)}, bf16[48,32,512]{2,1,0:T(8,128)(2,1)}, u32[]{:S(2)}, u32[]{:S(2)}) collective-permute-start(bf16[48,32,512]{2,1,0:T(8,128)(2,1)} %get-tuple-element.4.refs_2_.refs_12_), channel_id=1, source_target_pairs={{0,4},{1,5},{6,2},{7,3},{8,12},{9,13},{14,10},{15,11},{16,20},{17,... | collective-permute-start | bytes 4718600 | tf_op jit(solution)/shard_map/ppermute | solution.py:234
  13.7 27.4 %collective-permute-done.1.refs_4_.refs_14_ = bf16[48,32,512]{2,1,0:T(8,128)(2,1)S(1)} collective-permute-done((bf16[48,32,512]{2,1,0:T(8,128)(2,1)}, bf16[48,32,512]{2,1,0:T(8,128)(2,1)S(1)}, u32[]{:S(2)}, u32[]{:S(2)}) %collective-permute-start.1) | collective-permute-done | bytes 1572896 | tf_op jit(solution)/shard_map/ppermute | solution.py:234
  41.1 0.0 copy-start
  41.1 0.1 slice.16
  41.2 1.8 %collective-permute-start.5 = (bf16[24,32,512]{2,1,0:T(8,128)(2,1)S(1)}, bf16[24,32,512]{2,1,0:T(8,128)(2,1)S(1)}, u32[]{:S(2)}, u32[]{:S(2)}) collective-permute-start(bf16[24,32,512]{2,1,0:T(8,128)(2,1)S(1)} %slice.16), channel_id=1, source_target_pairs={{0,16},{1,17},{2,18},{3,19},{4,20},{5,21},{6,22},{7,23},{8,24},{9,... | collective-permute-start | bytes 2359304 | tf_op jit(solution)/shard_map/ppermute | solution.py:234
  43.0 0.0 collective-permute-done.3.refs_6_.refs_16_
  43.0 0.0 copy-start.1
  43.0 0.1 slice.17
  43.1 1.6 %collective-permute-start.6 = (bf16[24,32,512]{2,1,0:T(8,128)(2,1)S(1)}, bf16[24,32,512]{2,1,0:T(8,128)(2,1)S(1)}, u32[]{:S(2)}, u32[]{:S(2)}) collective-permute-start(bf16[24,32,512]{2,1,0:T(8,128)(2,1)S(1)} %slice.17), channel_id=1, source_target_pairs={{0,1},{1,0},{2,3},{3,2},{4,5},{5,4},{6,7},{7,6},{8,9},{9,8},{10,11... | collective-permute-start | bytes 2359304 | tf_op jit(solution)/shard_map/ppermute | solution.py:234
  44.6 0.0 copy-done.2
  44.6 0.0 collective-permute-start.10
  44.6 1.3 collective-permute-done.10
  46.0 0.6 collective-permute-start.11
  46.6 16.8 %collective-permute-done.11 = f32[48,512]{1,0:T(8,128)S(1)} collective-permute-done((f32[48,512]{1,0:T(8,128)S(1)}, f32[48,512]{1,0:T(8,128)S(1)}, u32[]{:S(2)}, u32[]{:S(2)}) %collective-permute-start.11) | collective-permute-done | bytes 98336 | tf_op jit(solution)/shard_map/ppermute | solution.py:234
  63.4 1.1 collective-permute-start.12
  64.5 1.7 %collective-permute-start.8 = (bf16[48,32,512]{2,1,0:T(8,128)(2,1)}, bf16[48,32,512]{2,1,0:T(8,128)(2,1)}, u32[]{:S(2)}, u32[]{:S(2)}) collective-permute-start(bf16[48,32,512]{2,1,0:T(8,128)(2,1)} %get-tuple-element.4.refs_2_.refs_12_), channel_id=1, source_target_pairs={{0,2},{1,3},{2,4},{3,5},{4,6},{5,7},{6,0},{7,1},{8,10},{9,11},{10,... | collective-permute-start | bytes 4718600 | tf_op jit(solution)/shard_map/ppermute | solution.py:234
  66.2 1.9 %collective-permute-done.12 = f32[48,512]{1,0:T(8,128)S(1)} collective-permute-done((f32[48,512]{1,0:T(8,128)S(1)}, f32[48,512]{1,0:T(8,128)S(1)}, u32[]{:S(2)}, u32[]{:S(2)}) %collective-permute-start.12) | collective-permute-done | bytes 98336 | tf_op jit(solution)/shard_map/ppermute | solution.py:234
  68.1 0.0 copy-start.3
  68.1 3.7 %collective-permute-start.15 = (f32[48,512]{1,0:T(8,128)S(1)}, f32[48,512]{1,0:T(8,128)S(1)}, u32[]{:S(2)}, u32[]{:S(2)}) collective-permute-start(f32[48,512]{1,0:T(8,128)S(1)} %add.30), channel_id=1, source_target_pairs={{0,6},{1,7},{2,0},{3,1},{4,2},{5,3},{6,4},{7,5},{8,14},{9,15},{10,... | collective-permute-start | bytes 294920 | tf_op jit(solution)/shard_map/ppermute | solution.py:234
  71.8 0.0 collective-permute-done.5
  71.8 0.0 collective-permute-start.14
  71.8 1.0 constant_dynamic-update-slice_fusion.1
  72.8 0.0 collective-permute-done.6
  72.8 1.1 collective-permute-start.13
  73.9 1.0 constant_dynamic-update-slice_fusion.refs_8_.refs_18_
  74.9 27.3 %collective-permute-done.15 = f32[48,512]{1,0:T(8,128)S(1)} collective-permute-done((f32[48,512]{1,0:T(8,128)S(1)}, f32[48,512]{1,0:T(8,128)S(1)}, u32[]{:S(2)}, u32[]{:S(2)}) %collective-permute-start.15) | collective-permute-done | bytes 98336 | tf_op jit(solution)/shard_map/ppermute | solution.py:234
  102.2 0.0 collective-permute-start
  102.2 6.7 %collective-permute-done.14 = f32[48,512]{1,0:T(8,128)S(1)} collective-permute-done((f32[48,512]{1,0:T(8,128)S(1)}, f32[48,512]{1,0:T(8,128)S(1)}, u32[]{:S(2)}, u32[]{:S(2)}) %collective-permute-start.14) | collective-permute-done | bytes 98336 | tf_op jit(solution)/shard_map/ppermute | solution.py:234
  108.9 0.0 copy-done.1
  108.9 0.0 collective-permute-start.4
  108.9 0.0 collective-permute-done.13
  108.9 0.0 copy-done
  108.9 0.5 collective-permute-start.2
  109.4 0.0 collective-permute-done.9.refs_11_.refs_21_
  109.4 0.1 collective-permute-start.7
  109.5 0.0 copy-done.3
  109.5 0.6 dynamic_slice.8.refs_1_
  110.1 1.2 dynamic-slice_bitcast_fusion.refs_0_
  111.4 0.6 reshape.11.refs_23_
  112.0 0.6 reshape.10.refs_22_
  112.6 0.0 collective-permute-done.8.refs_10_.refs_20_
  112.6 0.0 collective-permute-done.refs_3_.refs_13_
  112.6 0.0 collective-permute-done.4.refs_7_.refs_17_
  112.6 2.1 %collective-permute-done.2.refs_5_.refs_15_ = bf16[48,32,512]{2,1,0:T(8,128)(2,1)} collective-permute-done((bf16[48,32,512]{2,1,0:T(8,128)(2,1)S(1)}, bf16[48,32,512]{2,1,0:T(8,128)(2,1)}, u32[]{:S(2)}, u32[]{:S(2)}) %collective-permute-start.2) | collective-permute-done | bytes 1572896 | tf_op jit(solution)/shard_map/ppermute | solution.py:234
  114.7 2.2 %collective-permute-done.7.refs_9_.refs_19_ = bf16[48,32,512]{2,1,0:T(8,128)(2,1)} collective-permute-done((bf16[48,32,512]{2,1,0:T(8,128)(2,1)}, bf16[48,32,512]{2,1,0:T(8,128)(2,1)}, u32[]{:S(2)}, u32[]{:S(2)}) %collective-permute-start.7) | collective-permute-done | bytes 1572896 | tf_op jit(solution)/shard_map/ppermute | solution.py:234
  117.0 13.2 %tiles.1 = f32[32,8,128]{2,1,0:T(8,128)} custom-call(s32[10]{0:T(128)} %dynamic-slice_bitcast_fusion.refs_0_, f32[1]{0:T(128)} %dynamic_slice.8.refs_1_, bf16[48,32,512]{2,1,0:T(8,128)(2,1)} %get-tuple-element.4.refs_2_.refs_12_, bf16[48,32,512]{2,1,0:T(8,128)(2,1)} %collective-permute-done.refs_3_.refs_13_, bf16[48,32,512]{2,1,0:T(8,128)(2,1)} %copy-done, ...), custom_call_target="tpu_custom_call" | custom-call | tf_op jit(solution)/shard_map/tiles/pallas_call | solution.py:171
  130.2 11.1 %all_to_all.5.refs_0_ = f32[32,8,128]{2,1,0:T(8,128)} all-to-all(f32[32,8,128]{2,1,0:T(8,128)} %tiles.1), channel_id=1, replica_groups=mesh['row'=4,'col'=8] {'row','col'}, dimensions={0} | all-to-all | bytes 262144 | tf_op jit(solution)/shard_map/all_to_all | solution.py:304
  141.3 1.8 %finish.1 = (f32[32,30]{1,0:T(8,128)}, f32[5,6]{1,0:T(8,128)}) custom-call(f32[32,8,128]{2,1,0:T(8,128)} %all_to_all.5.refs_0_), custom_call_target="tpu_custom_call" | custom-call | tf_op jit(solution)/shard_map/finish/pallas_call | solution.py:218
  (6 shorter events, 0.1 us)
Async XLA Ops:
  3.5 41.1 %copy-start.2 = (f32[48,512]{1,0:T(8,128)S(1)}, f32[48,512]{1,0:T(8,128)}, u32[]{:S(2)}) copy-start(f32[48,512]{1,0:T(8,128)} %get-tuple-element.5) | copy-start | bytes 294916
  3.5 37.6 %collective-permute-start.1 = (bf16[48,32,512]{2,1,0:T(8,128)(2,1)}, bf16[48,32,512]{2,1,0:T(8,128)(2,1)S(1)}, u32[]{:S(2)}, u32[]{:S(2)}) collective-permute-start(bf16[48,32,512]{2,1,0:T(8,128)(2,1)} %get-tuple-element.4.refs_2_.refs_12_), channel_id=1, source_target_pairs={{0,1},{1,0},{2,3},{3,2},{4,5},{5,4},{6,7},{7,6},{8,9},{9,8},{10,11... | collective-permute-start | bytes 4718600 | tf_op jit(solution)/shard_map/ppermute | solution.py:234
  6.5 36.5 %collective-permute-start.3 = (bf16[48,32,512]{2,1,0:T(8,128)(2,1)}, bf16[48,32,512]{2,1,0:T(8,128)(2,1)S(1)}, u32[]{:S(2)}, u32[]{:S(2)}) collective-permute-start(bf16[48,32,512]{2,1,0:T(8,128)(2,1)} %get-tuple-element.4.refs_2_.refs_12_), channel_id=1, source_target_pairs={{0,16},{1,17},{2,18},{3,19},{4,20},{5,21},{6,22},{7,23},{8,24},{9,... | collective-permute-start | bytes 4718600 | tf_op jit(solution)/shard_map/ppermute | solution.py:234
  8.0 101.4 %collective-permute-start.9 = (bf16[48,32,512]{2,1,0:T(8,128)(2,1)}, bf16[48,32,512]{2,1,0:T(8,128)(2,1)}, u32[]{:S(2)}, u32[]{:S(2)}) collective-permute-start(bf16[48,32,512]{2,1,0:T(8,128)(2,1)} %get-tuple-element.4.refs_2_.refs_12_), channel_id=1, source_target_pairs={{0,4},{1,5},{6,2},{7,3},{8,12},{9,13},{14,10},{15,11},{16,20},{17,... | collective-permute-start | bytes 4718600 | tf_op jit(solution)/shard_map/ppermute | solution.py:234
  41.1 67.8 %copy-start = (bf16[48,32,512]{2,1,0:T(8,128)(2,1)}, bf16[48,32,512]{2,1,0:T(8,128)(2,1)S(1)}, u32[]{:S(2)}) copy-start(bf16[48,32,512]{2,1,0:T(8,128)(2,1)S(1)} %collective-permute-done.1.refs_4_.refs_14_) | copy-start | bytes 4718596
  41.2 30.6 %collective-permute-start.5 = (bf16[24,32,512]{2,1,0:T(8,128)(2,1)S(1)}, bf16[24,32,512]{2,1,0:T(8,128)(2,1)S(1)}, u32[]{:S(2)}, u32[]{:S(2)}) collective-permute-start(bf16[24,32,512]{2,1,0:T(8,128)(2,1)S(1)} %slice.16), channel_id=1, source_target_pairs={{0,16},{1,17},{2,18},{3,19},{4,20},{5,21},{6,22},{7,23},{8,24},{9,... | collective-permute-start | bytes 2359304 | tf_op jit(solution)/shard_map/ppermute | solution.py:234
  43.0 65.9 %copy-start.1 = (bf16[48,32,512]{2,1,0:T(8,128)(2,1)}, bf16[48,32,512]{2,1,0:T(8,128)(2,1)S(1)}, u32[]{:S(2)}) copy-start(bf16[48,32,512]{2,1,0:T(8,128)(2,1)S(1)} %collective-permute-done.3.refs_6_.refs_16_) | copy-start | bytes 4718596
  43.1 29.7 %collective-permute-start.6 = (bf16[24,32,512]{2,1,0:T(8,128)(2,1)S(1)}, bf16[24,32,512]{2,1,0:T(8,128)(2,1)S(1)}, u32[]{:S(2)}, u32[]{:S(2)}) collective-permute-start(bf16[24,32,512]{2,1,0:T(8,128)(2,1)S(1)} %slice.17), channel_id=1, source_target_pairs={{0,1},{1,0},{2,3},{3,2},{4,5},{5,4},{6,7},{7,6},{8,9},{9,8},{10,11... | collective-permute-start | bytes 2359304 | tf_op jit(solution)/shard_map/ppermute | solution.py:234
  44.6 1.3 collective-permute-start.10
  46.0 17.4 %collective-permute-start.11 = (f32[48,512]{1,0:T(8,128)S(1)}, f32[48,512]{1,0:T(8,128)S(1)}, u32[]{:S(2)}, u32[]{:S(2)}) collective-permute-start(f32[48,512]{1,0:T(8,128)S(1)} %add.28), channel_id=1, source_target_pairs={{0,1},{1,0},{2,3},{3,2},{4,5},{5,4},{6,7},{7,6},{8,9},{9,8},{10,11... | collective-permute-start | bytes 294920 | tf_op jit(solution)/shard_map/ppermute | solution.py:234
  63.4 4.7 %collective-permute-start.12 = (f32[48,512]{1,0:T(8,128)S(1)}, f32[48,512]{1,0:T(8,128)S(1)}, u32[]{:S(2)}, u32[]{:S(2)}) collective-permute-start(f32[48,512]{1,0:T(8,128)S(1)} %add.29), channel_id=1, source_target_pairs={{0,16},{1,17},{2,18},{3,19},{4,20},{5,21},{6,22},{7,23},{8,24},{9,... | collective-permute-start | bytes 294920 | tf_op jit(solution)/shard_map/ppermute | solution.py:234
  64.5 48.1 %collective-permute-start.8 = (bf16[48,32,512]{2,1,0:T(8,128)(2,1)}, bf16[48,32,512]{2,1,0:T(8,128)(2,1)}, u32[]{:S(2)}, u32[]{:S(2)}) collective-permute-start(bf16[48,32,512]{2,1,0:T(8,128)(2,1)} %get-tuple-element.4.refs_2_.refs_12_), channel_id=1, source_target_pairs={{0,2},{1,3},{2,4},{3,5},{4,6},{5,7},{6,0},{7,1},{8,10},{9,11},{10,... | collective-permute-start | bytes 4718600 | tf_op jit(solution)/shard_map/ppermute | solution.py:234
  68.1 41.4 %copy-start.3 = (f32[32]{0:T(128)S(1)}, f32[32]{0:T(128)}, u32[]{:S(2)}) copy-start(f32[32]{0:T(128)} %constant.23.clone) | copy-start | bytes 388
  68.1 34.1 %collective-permute-start.15 = (f32[48,512]{1,0:T(8,128)S(1)}, f32[48,512]{1,0:T(8,128)S(1)}, u32[]{:S(2)}, u32[]{:S(2)}) collective-permute-start(f32[48,512]{1,0:T(8,128)S(1)} %add.30), channel_id=1, source_target_pairs={{0,6},{1,7},{2,0},{3,1},{4,2},{5,3},{6,4},{7,5},{8,14},{9,15},{10,... | collective-permute-start | bytes 294920 | tf_op jit(solution)/shard_map/ppermute | solution.py:234
  71.8 37.1 %collective-permute-start.14 = (f32[48,512]{1,0:T(8,128)S(1)}, f32[48,512]{1,0:T(8,128)S(1)}, u32[]{:S(2)}, u32[]{:S(2)}) collective-permute-start(f32[48,512]{1,0:T(8,128)S(1)} %add.30), channel_id=1, source_target_pairs={{0,4},{1,5},{2,6},{3,7},{4,0},{5,1},{6,2},{7,3},{8,12},{9,13},{10,... | collective-permute-start | bytes 294920 | tf_op jit(solution)/shard_map/ppermute | solution.py:234
  72.8 36.2 %collective-permute-start.13 = (f32[48,512]{1,0:T(8,128)S(1)}, f32[48,512]{1,0:T(8,128)S(1)}, u32[]{:S(2)}, u32[]{:S(2)}) collective-permute-start(f32[48,512]{1,0:T(8,128)S(1)} %add.30), channel_id=1, source_target_pairs={{0,2},{1,3},{2,4},{3,5},{4,6},{5,7},{6,0},{7,1},{8,10},{9,11},{10,... | collective-permute-start | bytes 294920 | tf_op jit(solution)/shard_map/ppermute | solution.py:234
  102.2 10.4 %collective-permute-start = (bf16[48,32,512]{2,1,0:T(8,128)(2,1)}, bf16[48,32,512]{2,1,0:T(8,128)(2,1)}, u32[]{:S(2)}, u32[]{:S(2)}) collective-permute-start(bf16[48,32,512]{2,1,0:T(8,128)(2,1)} %get-tuple-element.4.refs_2_.refs_12_), channel_id=1, source_target_pairs={{0,8},{1,9},{2,10},{3,11},{4,12},{5,13},{6,14},{7,15},{8,0},{9,1},... | collective-permute-start | bytes 4718600 | tf_op jit(solution)/shard_map/ppermute | solution.py:234
  108.9 3.7 %collective-permute-start.4 = (bf16[48,32,512]{2,1,0:T(8,128)(2,1)S(1)}, bf16[48,32,512]{2,1,0:T(8,128)(2,1)}, u32[]{:S(2)}, u32[]{:S(2)}) collective-permute-start(bf16[48,32,512]{2,1,0:T(8,128)(2,1)S(1)} %collective-permute-done.3.refs_6_.refs_16_), channel_id=1, source_target_pairs={{0,8},{1,9},{2,10},{3,11},{4,12},{5,13},{6,14},{7,15},{8,0},{9,1},... | collective-permute-start | bytes 4718600 | tf_op jit(solution)/shard_map/ppermute | solution.py:234
  108.9 5.8 %collective-permute-start.2 = (bf16[48,32,512]{2,1,0:T(8,128)(2,1)S(1)}, bf16[48,32,512]{2,1,0:T(8,128)(2,1)}, u32[]{:S(2)}, u32[]{:S(2)}) collective-permute-start(bf16[48,32,512]{2,1,0:T(8,128)(2,1)S(1)} %collective-permute-done.1.refs_4_.refs_14_), channel_id=1, source_target_pairs={{0,8},{1,9},{2,10},{3,11},{4,12},{5,13},{6,14},{7,15},{8,0},{9,1},... | collective-permute-start | bytes 4718600 | tf_op jit(solution)/shard_map/ppermute | solution.py:234
  109.4 7.5 %collective-permute-start.7 = (bf16[48,32,512]{2,1,0:T(8,128)(2,1)}, bf16[48,32,512]{2,1,0:T(8,128)(2,1)}, u32[]{:S(2)}, u32[]{:S(2)}) collective-permute-start(bf16[48,32,512]{2,1,0:T(8,128)(2,1)} %constant_dynamic-update-slice_fusion.refs_8_.refs_18_), channel_id=1, source_target_pairs={{0,8},{1,9},{2,10},{3,11},{4,12},{5,13},{6,14},{7,15},{8,0},{9,1},... | collective-permute-start | bytes 4718600 | tf_op jit(solution)/shard_map/ppermute | solution.py:234

commit v2 on v1

v2 whole, which is shorter than its diff:
```python
import math

import jax
import jax.numpy as jnp
import numpy as np
from jax import lax
from jax.experimental import pallas as pl
from jax.experimental.pallas import tpu as pltpu
from jax.sharding import PartitionSpec as P


AXES = ("row", "col")
NT = (((1,), (1,)), ((), ()))


class Grid:
    def __init__(self, mesh):
        devices = mesh.devices
        rows, cols = devices.shape
        flat = list(devices.flat)
        places = [getattr(d, "coords", None) for d in flat]
        if all(p is not None for p in places):
            at = [(*p[:3], getattr(d, "core_on_chip", 0)) for p, d in zip(places, flat)]
        else:
            at = [(0, r, c, 0) for r in range(rows) for c in range(cols)]
        levels = [sorted({a[k] for a in at}) for k in range(4)]
        self.at = [tuple(levels[k].index(a[k]) for k in range(4)) for a in at]
        self.size = tuple(len(v) for v in levels)
        self.index = {a: i for i, a in enumerate(self.at)}
        if len(self.index) != len(flat) or len(flat) != math.prod(self.size):
            self.at = [(0, r, c, 0) for r in range(rows) for c in range(cols)]
            self.size = (1, rows, cols, 1)
            self.index = {a: i for i, a in enumerate(self.at)}

    def moved(self, i, shift):
        return self.index[tuple((p + s) % n for p, s, n in zip(self.at[i], shift, self.size))]

    def pairs(self, shift, senders=None):
        return [(i, self.moved(i, shift)) for i in range(len(self.at)) if senders is None or senders(self.at[i])]


def pack_kernel(kt, kv, width, start, text_ref, vision_ref, packed_ref, sums_ref):
    for k in range(kt * text_ref.shape[0], start):
        packed_ref[k] = jnp.zeros(packed_ref.shape[1:], packed_ref.dtype)
        sums_ref[pl.ds(k, 1), :] = jnp.zeros((1, width), jnp.float32)
    for ref, per, first in ((text_ref, kt, 0), (vision_ref, kv, start)):
        for layer in range(ref.shape[0]):
            for k in range(per):
                values = ref[layer, :, k * width : (k + 1) * width]
                packed_ref[first + layer * per + k] = values
                sums_ref[pl.ds(first + layer * per + k, 1), :] = jnp.sum(
                    values.astype(jnp.float32), axis=0, keepdims=True
                )


def pack(text, vision, kt, kv, width, start):
    chunks = start + kv * vision.shape[0]
    rows = text.shape[1]
    return pl.pallas_call(
        lambda *refs: pack_kernel(kt, kv, width, start, *refs),
        out_shape=(
            jax.ShapeDtypeStruct((chunks, rows, width), text.dtype),
            jax.ShapeDtypeStruct((chunks, width), jnp.float32),
        ),
        name="pack",
    )(text, vision)


def centered_rows(refs, mean_ref, first, per, count, out_ref, layer):
    rows, width = refs[0].shape[1:]
    for k in range(per):
        mean = mean_ref[pl.ds(first + k, 1), :] * (1.0 / count)
        for j, ref in enumerate(refs):
            out_ref[layer, pl.ds(j * rows, rows), pl.ds(k * width, width)] = (
                ref[k].astype(jnp.float32) - mean
            ).astype(jnp.bfloat16)


def add_products(la, lb, ks, gs, low, rows_ref, cols_ref):
    pairs = la * lb
    for a in range(la):
        for b in range(lb):
            prod = ks[a] * gs[b]
            rows_ref[pl.ds(a * lb + b, 1), :] = jnp.sum(prod[low:], axis=0, keepdims=True)
            cols_ref[:, pl.ds(a * lb + b, 1)] = jnp.sum(prod, axis=1, keepdims=True)
    for n, refs in ((pairs, ks), (pairs + la, gs)):
        for i in range(refs.shape[0]):
            cols_ref[:, pl.ds(n + i, 1)] = jnp.sum(refs[i] * refs[i], axis=1, keepdims=True)


def region_kernel(geo, na, nb, mean_ref, *refs):
    la, lb, kt, kv, start, rows, count = geo
    n = na + nb
    text, vision = refs[:n], refs[n : 2 * n]
    text_out, vision_out, rows_out, cols_out, bt, bv, ks, gs = refs[2 * n :]
    step = pl.program_id(0)

    def layer(blocks, per, first, out, bc, store):
        centered_rows(blocks[:na], mean_ref, first, per, count, out, 0)
        centered_rows(blocks[na:], mean_ref, first, per, count, bc, 0)
        store[step] = lax.dot_general(bc[0], out[0], NT, preferred_element_type=jnp.float32)

    @pl.when(step < la)
    def _():
        layer(text, kt, step * kt, text_out, bt, ks)

    @pl.when(step < lb)
    def _():
        layer(vision, kv, start + step * kv, vision_out, bv, gs)

    @pl.when(step == max(la, lb) - 1)
    def _():
        rows_out[...] = jnp.zeros_like(rows_out)
        cols_out[...] = jnp.zeros_like(cols_out)
        add_products(la, lb, ks, gs, rows, rows_out, cols_out)


def layer_specs(geo, n):
    la, lb, kt, kv, start, rows, _ = geo

    def of(width):
        text = pl.BlockSpec((kt, rows, width), lambda i: (jnp.minimum(i, la - 1), 0, 0))
        vision = pl.BlockSpec((kv, rows, width), lambda i: (start // kv + jnp.minimum(i, lb - 1), 0, 0))
        return [text] * n + [vision] * n

    return of


def region(geo, a_blocks, b_blocks, totals):
    la, lb, kt, kv, _, rows, _ = geo
    na, nb = len(a_blocks), len(b_blocks)
    width = totals.shape[-1]
    blocks = [*a_blocks, *b_blocks]
    return pl.pallas_call(
        lambda *refs: region_kernel(geo, na, nb, *refs),
        grid=(max(la, lb),),
        in_specs=[pl.BlockSpec(totals.shape, lambda i: (0, 0))] + layer_specs(geo, na + nb)(width),
        out_specs=[
            pl.BlockSpec((1, na * rows, kt * width), lambda i: (jnp.minimum(i, la - 1), 0, 0)),
            pl.BlockSpec((1, na * rows, kv * width), lambda i: (jnp.minimum(i, lb - 1), 0, 0)),
            pl.BlockSpec((8 * (128 // rows), na * rows), lambda i: (0, 0)),
            pl.BlockSpec((nb * rows, 128), lambda i: (0, 0)),
        ],
        out_shape=(
            jax.ShapeDtypeStruct((la, na * rows, kt * width), jnp.bfloat16),
            jax.ShapeDtypeStruct((lb, na * rows, kv * width), jnp.bfloat16),
            jax.ShapeDtypeStruct((8 * (128 // rows), na * rows), jnp.float32),
            jax.ShapeDtypeStruct((nb * rows, 128), jnp.float32),
        ),
        scratch_shapes=[
            pltpu.VMEM((1, nb * rows, kt * width), jnp.bfloat16),
            pltpu.VMEM((1, nb * rows, kv * width), jnp.bfloat16),
            pltpu.VMEM((la, nb * rows, na * rows), jnp.float32),
            pltpu.VMEM((lb, nb * rows, na * rows), jnp.float32),
        ],
        cost_estimate=pl.CostEstimate(flops=4_000_000_000, bytes_accessed=16_000_000, transcendentals=0),
        compiler_params=pltpu.CompilerParams(vmem_limit_bytes=56 * 1024 * 1024),
    )(totals, *blocks, *blocks)


def last_kernel(geo, parts, nb, ndest, dest_ref, weight_ref, mean_ref, *refs):
    la, lb, kt, kv, start, rows, count = geo
    npart = len(parts)
    last_text, last_vision = refs[0], refs[1]
    texts, visions = refs[2 : 2 + npart], refs[2 + npart : 2 + 2 * npart]
    part_rows = refs[2 + 2 * npart : 2 + 3 * npart]
    part_cols = refs[2 + 3 * npart : 2 + 4 * npart]
    payload_ref = refs[2 + 4 * npart]
    ct, cv, ks, gs, rows_ref, cols_ref, all_ref = refs[3 + 4 * npart :]
    step = pl.program_id(0)

    def layer(block, per, first, centered, others, store):
        centered_rows([block], mean_ref, first, per, count, centered, 0)
        at = 0
        for other in others:
            size = other.shape[1]
            store[step, :, at : at + size] = lax.dot_general(
                centered[0], other[0], NT, preferred_element_type=jnp.float32
            )
            at += size

    @pl.when(step < la)
    def _():
        layer(last_text, kt, step * kt, ct, texts, ks)

    @pl.when(step < lb)
    def _():
        layer(last_vision, kv, start + step * kv, cv, visions, gs)

    @pl.when(step == max(la, lb) - 1)
    def _():
        pairs = la * lb
        wlast = weight_ref[0]
        rows_ref[...] = jnp.zeros_like(rows_ref)
        cols_ref[...] = jnp.zeros_like(cols_ref)
        add_products(la, lb, ks, gs, 0, rows_ref, cols_ref)
        at = 0
        for ref in part_rows:
            size = ref.shape[1]
            rows_ref[:, at : at + size] = ref[...] + wlast * rows_ref[:, at : at + size]
            at += size
        early = part_cols[0][...]
        for ref in part_cols[1:]:
            early = early + ref[...]
        all_ref[...] = jnp.zeros_like(all_ref)
        all_ref[0 : (nb + 1) * rows - rows, :] = early
        all_ref[nb * rows : (nb + 1) * rows, :] = wlast * cols_ref[...]
        by_pair = all_ref[...].T
        sub_t = lax.broadcasted_iota(jnp.int32, (128, 128), 0)
        cell = jnp.where(sub_t < rows, 1.0, 2.0)
        totals = jnp.sum(all_ref[...] * cell, axis=0, keepdims=True)
        sub = lax.broadcasted_iota(jnp.int32, (8, 128), 0)
        lane8 = lax.broadcasted_iota(jnp.int32, (8, 128), 1)
        spot = (lane8 // rows) * 8 + sub
        own = lane8 % rows
        spread = jnp.broadcast_to(totals, (8, 128))

        def shifted(x, by):
            by %= 128
            return pltpu.roll(x, by, 1) if by else x

        q_cross, q_self = pairs // 8, (pairs + 1) // 8
        base = jnp.zeros((8, 128), jnp.float32)
        base = jnp.where((spot == pairs) & (own < pairs), shifted(spread, q_cross * rows), base)
        base = jnp.where((spot == pairs + 1) & (own < la + lb), shifted(spread, q_self * rows - pairs), base)
        for d in range(ndest):
            payload_ref[d] = base
        na = rows_ref.shape[1] // rows
        for j in range(na + nb):
            tile = base
            for q in range(128 // rows):
                if j < na:
                    c0 = j * rows
                    part = shifted(
                        rows_ref[8 * q : 8 * q + 8, c0 // 128 * 128 : c0 // 128 * 128 + 128], q * rows - c0 % 128
                    )
                    if j == 0:
                        part = part + shifted(by_pair[8 * q : 8 * q + 8, :], q * rows)
                else:
                    part = shifted(by_pair[8 * q : 8 * q + 8, :], (q - (j - na + 1)) * rows)
                tile = jnp.where((lane8 // rows == q) & (spot < pairs), part, tile)
            payload_ref[dest_ref[j]] = tile


def last(geo, parts, last_block, nb, totals, dest, weight, ndest):
    la, lb, kt, kv, _, rows, _ = geo
    width = totals.shape[-1]
    na_rows = sum(p[2].shape[1] for p in parts)
    assert (nb + 1) * rows <= 128 and 128 % rows == 0 and na_rows % 128 == 0
    assert 8 * (128 // rows) >= la * lb + 2 and la * lb + la + lb <= 128 and la * lb <= rows
    smem = pl.BlockSpec(memory_space=pltpu.SMEM)
    whole = lambda shape: pl.BlockSpec(shape, lambda i: (0,) * len(shape))
    texts, visions, part_rows, part_cols = zip(*parts)
    return pl.pallas_call(
        lambda *refs: last_kernel(geo, parts, nb, ndest, *refs),
        grid=(max(la, lb),),
        in_specs=[smem, smem, whole(totals.shape)]
        + layer_specs(geo, 1)(width)
        + [pl.BlockSpec((1, *t.shape[1:]), lambda i: (jnp.minimum(i, la - 1), 0, 0)) for t in texts]
        + [pl.BlockSpec((1, *v.shape[1:]), lambda i: (jnp.minimum(i, lb - 1), 0, 0)) for v in visions]
        + [whole(x.shape) for x in (*part_rows, *part_cols)],
        out_specs=whole((ndest, 8, 128)),
        out_shape=jax.ShapeDtypeStruct((ndest, 8, 128), jnp.float32),
        scratch_shapes=[
            pltpu.VMEM((1, rows, kt * width), jnp.bfloat16),
            pltpu.VMEM((1, rows, kv * width), jnp.bfloat16),
            pltpu.VMEM((la, rows, na_rows), jnp.float32),
            pltpu.VMEM((lb, rows, na_rows), jnp.float32),
            pltpu.VMEM((8 * (128 // rows), na_rows), jnp.float32),
            pltpu.VMEM((rows, 128), jnp.float32),
            pltpu.VMEM((128, 128), jnp.float32),
        ],
        compiler_params=pltpu.CompilerParams(vmem_limit_bytes=56 * 1024 * 1024),
        name="last",
    )(dest, weight, totals, last_block, last_block, *texts, *visions, *part_rows, *part_cols)


def finish_kernel(la, lb, rows, count, in_ref, terms_ref, cka_ref):
    pairs = la * lb
    total = jnp.sum(in_ref[...], axis=0)
    spots = jnp.concatenate([total[:, q * rows : (q + 1) * rows] for q in range(128 // rows)], axis=0)
    cross = spots[pairs : pairs + 1, :]
    selves = jnp.broadcast_to(spots[pairs + 1 : pairs + 2, :], (rows, rows)).T
    sub = lax.broadcasted_iota(jnp.int32, (rows, rows), 0)
    lane = lax.broadcasted_iota(jnp.int32, (rows, rows), 1)
    text = jnp.sum(jnp.where(sub == lane // lb, selves, 0.0), axis=0, keepdims=True)
    vision = jnp.sum(jnp.where(sub == la + lane % lb, selves, 0.0), axis=0, keepdims=True)
    inside = lax.broadcasted_iota(jnp.int32, (1, rows), 1) < pairs
    scale = 1.0 / jnp.sqrt(jnp.where(inside, text * vision, 1.0))
    terms = spots.T * (scale * count) if spots.shape[0] == rows else spots.T[:, :rows] * (scale * count)
    terms_ref[...] = terms[:, :pairs]
    cka = cross * scale
    for a in range(la):
        cka_ref[a : a + 1, :] = cka[:, a * lb : (a + 1) * lb]


def finish(received, la, lb, rows, count):
    return pl.pallas_call(
        lambda *refs: finish_kernel(la, lb, rows, count, *refs),
        out_shape=(
            jax.ShapeDtypeStruct((rows, la * lb), jnp.float32),
            jax.ShapeDtypeStruct((la, lb), jnp.float32),
        ),
        name="finish",
    )(received)


def solution(mesh):
    grid = Grid(mesh)
    nx, ny, nz, nc = grid.size
    assert nz % 2 == 0
    ndev = len(grid.at)

    def send(value, shift, senders=None):
        return lax.ppermute(value, AXES, grid.pairs(shift, senders))

    def half_sender(place):
        z = place[2]
        return (z < nz // 2) == ((z % (nz // 2)) % 2 == 0)

    def body(text, vision):
        la, rows, da = text.shape
        lb, _, db = vision.shape
        count = rows * ndev
        width = math.gcd(da, db)
        kt, kv = da // width, db // width
        start = -(-la * kt // kv) * kv
        me = lax.axis_index(AXES)
        own, sums = pack(text, vision, kt, kv, width, start)
        chunks = own.shape[0]

        geo = (la, lb, kt, kv, start, rows, count)
        full_shifts = range(1, (nz + 1) // 2)
        b_blocks = [own] + [send(own, (0, 0, d, 0)) for d in full_shifts]
        b_shifts = [(0, 0, d, 0) for d in full_shifts]

        for k in (3, 0, 1, 2):
            part = sums
            for d in range(1, grid.size[k]):
                shift = tuple(d if i == k else 0 for i in range(4))
                arrived = send(part, shift)
                sums = sums + arrived

        def with_cores(block, dx, dy):
            out = [(block, (dx, dy, 0, 0))]
            for dc in range(1, nc):
                out.append((send(block, (0, 0, 0, dc)), (dx, dy, 0, dc)))
            return out

        plane = {(0, 0): own}
        for d in range(1, nx):
            plane[d, 0] = send(own, (d, 0, 0, 0))
        for d in range(1, ny):
            plane[0, d] = send(own, (0, d, 0, 0))
        early = [pair for (dx, dy), block in plane.items() for pair in with_cores(block, dx, dy)]
        half = chunks // 2
        late = []
        for dx in range(1, nx):
            for dy in range(1, ny):
                first = send(plane[dx, 0][:half], (0, dy, 0, 0))
                second = send(plane[0, dy][half:], (dx, 0, 0, 0))
                late += with_cores(jnp.concatenate([first, second], axis=0), dx, dy)

        weight = np.zeros((ndev,), np.float32)
        last_block = send(own, (0, 0, nz // 2, 0), half_sender)
        b_shifts.append((0, 0, nz // 2, 0))
        for i in range(ndev):
            if half_sender(grid.at[i]):
                weight[grid.moved(i, (0, 0, nz // 2, 0))] = 1.0
        shifts = [s for _, s in early + late] + b_shifts
        table = np.array(
            [[grid.moved(i, tuple(-s for s in shift)) for shift in shifts] for i in range(ndev)], np.int32
        )
        dest = lax.dynamic_index_in_dim(jnp.asarray(table), me, 0, keepdims=False)
        w = lax.dynamic_slice(jnp.asarray(weight), (me,), (1,))
        parts = [region(geo, [x for x, _ in early], b_blocks, sums)]
        if late:
            parts.append(region(geo, [x for x, _ in late], b_blocks, sums))
        payload = last(geo, parts, last_block, len(b_blocks), sums, dest, w, ndev)
        received = lax.all_to_all(payload, AXES, 0, 0, tiled=True)
        return finish(received, la, lb, rows, count)

    spec = P(None, AXES, None)
    return jax.shard_map(body, mesh=mesh, in_specs=(spec, spec), out_specs=(P(AXES, None), P()), check_vma=False)
```

time: 143 us -> 182 us (1.27)
  waiting for transfers between devices: 85.8 us -> 110 us
  Pallas kernels: 17.9 us -> 35.4 us
  starting transfers between devices: 22.3 us -> 16.3 us
  blocking collectives: 11.1 us -> 13.3 us
    ppermute x16, waiting for transfers between devices: 85.8 us -> 110 us  [send(): return lax.ppermute(value, AXES, grid.pairs(shift, senders))]
    pallas_call x1 -> x3, Pallas kernels: 13.2 us -> 30.8 us  [the longest x2 20.2 us: region(): pl.pallas_call(lambda *refs: region_kernel(geo, na, nb, *refs), grid=(max...]
    ppermute x16, starting transfers between devices: 22.3 us -> 16.3 us  [send(): return lax.ppermute(value, AXES, grid.pairs(shift, senders))]
    all_to_all x1, blocking collectives: 11.1 us -> 13.3 us  [body(): received = lax.all_to_all(payload, AXES, 0, 0, tiled=True)]
  transfers between devices with their start and end apart: 16 -> 16, of which waited for: 8 -> 8; matrix products, arithmetic and copies ran while one was open for 4% -> 3% of each run, Pallas kernels for 0% -> 11%
where the time goes in v2:
time: 182 us; the launch traced here: 181 us
  waiting for transfers between devices  110 us (60%)
  Pallas kernels  35.4 us (19%)
  starting transfers between devices  16.3 us (9%)
  blocking collectives  13.3 us (7%)
  local copies, waits for them, and re-layouts  5.07 us (3%)
    ppermute x16, waiting for transfers between devices, send(): return lax.ppermute(value, AXES, grid.pairs(shift, senders))  110 us
    pallas_call x2, Pallas kernels, region(): pl.pallas_call(lambda *refs: region_kernel(geo, na, nb, *refs), grid=(max...  20.2 us
    ppermute x16, starting transfers between devices, send(): return lax.ppermute(value, AXES, grid.pairs(shift, senders))  16.3 us
    all_to_all x1, blocking collectives, body(): received = lax.all_to_all(payload, AXES, 0, 0, tiled=True)  13.3 us
    pallas_call x1, Pallas kernels, last(): pl.pallas_call(lambda *refs: last_kernel(geo, parts, nb, ndest, *refs), g...  10.6 us
  transfers between devices with their start and end apart: 16, of which 8 were waited for; matrix products, arithmetic and copies ran while one was open for 3% of the time, Pallas kernels for 11%

profile of v2, /device:TPU:0, one launch (start us, length us, event | category | flops | bytes accessed | tf_op | source)
XLA Modules:
  0.0 181.5 jit_solution(12615952818750784697)
XLA Ops:
  0.6 2.9 %pack.1 = (bf16[48,32,512]{2,1,0:T(8,128)(2,1)}, f32[48,512]{1,0:T(8,128)}) custom-call(bf16[5,32,3584]{2,1,0:T(8,128)(2,1)} %refs_0_.1, bf16[6,32,1024]{2,1,0:T(8,128)(2,1)} %refs_1_.1), custom_call_target="tpu_custom_call" | custom-call | tf_op jit(solution)/shard_map/pack/pallas_call | solution.py:59
  3.5 0.0 copy-start.3
  3.5 3.0 %collective-permute-start.8 = (bf16[48,32,512]{2,1,0:T(8,128)(2,1)}, bf16[48,32,512]{2,1,0:T(8,128)(2,1)S(1)}, u32[]{:S(2)}, u32[]{:S(2)}) collective-permute-start(bf16[48,32,512]{2,1,0:T(8,128)(2,1)} %get-tuple-element.13.refs_1_.refs_7_.refs_9_.refs_15_.refs_3_), channel_id=1, source_target_pairs={{0,1},{1,0},{2,3},{3,2},{4,5},{5,4},{6,7},{7,6},{8,9},{9,8},{10,11... | collective-permute-start | bytes 4718600 | tf_op jit(solution)/shard_map/ppermute | solution.py:315
  6.5 1.5 collective-permute-start.10
  8.0 0.0 collective-permute-start.7
  8.0 33.1 %collective-permute-done.8.refs_3_.refs_11_ = bf16[48,32,512]{2,1,0:T(8,128)(2,1)S(1)} collective-permute-done((bf16[48,32,512]{2,1,0:T(8,128)(2,1)}, bf16[48,32,512]{2,1,0:T(8,128)(2,1)S(1)}, u32[]{:S(2)}, u32[]{:S(2)}) %collective-permute-start.8) | collective-permute-done | bytes 1572896 | tf_op jit(solution)/shard_map/ppermute | solution.py:315
  41.1 0.0 copy-start.1
  41.1 0.1 slice.8
  41.1 0.0 copy-start
  41.1 1.8 %collective-permute-start.13 = (bf16[24,32,512]{2,1,0:T(8,128)(2,1)S(1)}, bf16[24,32,512]{2,1,0:T(8,128)(2,1)S(1)}, u32[]{:S(2)}, u32[]{:S(2)}) collective-permute-start(bf16[24,32,512]{2,1,0:T(8,128)(2,1)S(1)} %slice.8), channel_id=1, source_target_pairs={{0,16},{1,17},{2,18},{3,19},{4,20},{5,21},{6,22},{7,23},{8,24},{9,... | collective-permute-start | bytes 2359304 | tf_op jit(solution)/shard_map/ppermute | solution.py:315
  43.0 0.0 collective-permute-done.10.refs_5_.refs_13_
  43.0 1.2 slice.9
  44.2 1.6 collective-permute-start.14
  45.7 0.0 copy-done.3
  45.7 0.0 collective-permute-start
  45.8 1.3 collective-permute-done
  47.1 0.6 collective-permute-start.1
  47.7 16.9 %collective-permute-done.1 = f32[48,512]{1,0:T(8,128)S(1)} collective-permute-done((f32[48,512]{1,0:T(8,128)S(1)}, f32[48,512]{1,0:T(8,128)S(1)}, u32[]{:S(2)}, u32[]{:S(2)}) %collective-permute-start.1) | collective-permute-done | bytes 98336 | tf_op jit(solution)/shard_map/ppermute | solution.py:315
  64.6 1.2 collective-permute-start.2
  65.9 3.4 %collective-permute-done.2 = f32[48,512]{1,0:T(8,128)S(1)} collective-permute-done((f32[48,512]{1,0:T(8,128)S(1)}, f32[48,512]{1,0:T(8,128)S(1)}, u32[]{:S(2)}, u32[]{:S(2)}) %collective-permute-start.2) | collective-permute-done | bytes 98336 | tf_op jit(solution)/shard_map/ppermute | solution.py:315
  69.3 0.0 copy-start.4
  69.3 3.7 %collective-permute-start.5 = (f32[48,512]{1,0:T(8,128)S(1)}, f32[48,512]{1,0:T(8,128)S(1)}, u32[]{:S(2)}, u32[]{:S(2)}) collective-permute-start(f32[48,512]{1,0:T(8,128)S(1)} %add.30), channel_id=1, source_target_pairs={{0,6},{1,7},{2,0},{3,1},{4,2},{5,3},{6,4},{7,5},{8,14},{9,15},{10,... | collective-permute-start | bytes 294920 | tf_op jit(solution)/shard_map/ppermute | solution.py:315
  73.0 0.0 collective-permute-start.4
  73.0 3.2 %collective-permute-done.5 = f32[48,512]{1,0:T(8,128)S(1)} collective-permute-done((f32[48,512]{1,0:T(8,128)S(1)}, f32[48,512]{1,0:T(8,128)S(1)}, u32[]{:S(2)}, u32[]{:S(2)}) %collective-permute-start.5) | collective-permute-done | bytes 98336 | tf_op jit(solution)/shard_map/ppermute | solution.py:315
  76.2 0.0 copy-done
  76.2 0.0 collective-permute-start.12
  76.2 35.7 %collective-permute-done.4 = f32[48,512]{1,0:T(8,128)S(1)} collective-permute-done((f32[48,512]{1,0:T(8,128)S(1)}, f32[48,512]{1,0:T(8,128)S(1)}, u32[]{:S(2)}, u32[]{:S(2)}) %collective-permute-start.4) | collective-permute-done | bytes 98336 | tf_op jit(solution)/shard_map/ppermute | solution.py:315
  111.9 0.0 copy-done.1
  111.9 0.0 collective-permute-start.9
  111.9 0.0 collective-permute-done.13
  111.9 0.5 collective-permute-start.11
  112.4 1.0 constant_dynamic-update-slice_fusion.1
  113.3 0.0 collective-permute-done.14
  113.3 0.0 collective-permute-start.3
  113.3 1.0 constant_dynamic-update-slice_fusion.refs_1_.refs_5_
  114.3 5.6 %collective-permute-done.3 = f32[48,512]{1,0:T(8,128)S(1)} collective-permute-done((f32[48,512]{1,0:T(8,128)S(1)}, f32[48,512]{1,0:T(8,128)S(1)}, u32[]{:S(2)}, u32[]{:S(2)}) %collective-permute-start.3) | collective-permute-done | bytes 98336 | tf_op jit(solution)/shard_map/ppermute | solution.py:315
  119.9 0.0 collective-permute-start.15
  119.9 0.0 collective-permute-done.7.refs_2_.refs_10_
  119.9 0.0 copy-start.2
  119.9 2.4 %collective-permute-start.6 = (bf16[48,32,512]{2,1,0:T(8,128)(2,1)S(1)}, bf16[48,32,512]{2,1,0:T(8,128)(2,1)}, u32[]{:S(2)}, u32[]{:S(2)}) collective-permute-start(bf16[48,32,512]{2,1,0:T(8,128)(2,1)S(1)} %copy-done), channel_id=1, source_target_pairs={{0,4},{1,5},{6,2},{7,3},{8,12},{9,13},{14,10},{15,11},{16,20},{17,... | collective-permute-start | bytes 4718600 | tf_op jit(solution)/shard_map/ppermute | solution.py:315
  122.3 0.0 copy-done.2
  122.3 0.0 copy-done.4
  122.4 0.6 dynamic_slice.8.refs_1_
  123.0 1.2 dynamic-slice_bitcast_fusion.refs_0_
  124.2 0.7 add_add_fusion.refs_0_.refs_2_
  124.9 0.0 collective-permute-done.12.refs_8_.refs_16_.refs_4_
  124.9 0.0 collective-permute-done.9.refs_4_.refs_12_
  124.9 0.0 collective-permute-done.11.refs_6_.refs_14_
  124.9 12.3 %shard_map.59 = (bf16[5,192,3584]{2,1,0:T(8,128)(2,1)}, bf16[6,192,1024]{2,1,0:T(8,128)(2,1)}, f32[32,192]{1,0:T(8,128)}, f32[64,128]{1,0:T(8,128)}) custom-call(f32[48,512]{1,0:T(8,128)} %add_add_fusion.refs_0_.refs_2_, bf16[48,32,512]{2,1,0:T(8,128)(2,1)} %get-tuple-element.13.refs_1_.refs_7_.refs_9_.refs_15_.refs_3_, bf16[48,32,512]{2,1,0:T(8,128)(2,1)} %copy-done.2, ...), custom_call_target="tpu_custom_call" | custom-call | flops 4000000000 | bytes 16000000 | tf_op jit(solution)/shard_map/pallas_call | solution.py:134
  137.2 0.0 collective-permute-done.15.refs_2_.refs_6_
  137.2 7.9 %shard_map.60 = (bf16[5,64,3584]{2,1,0:T(8,128)(2,1)}, bf16[6,64,1024]{2,1,0:T(8,128)(2,1)}, f32[32,64]{1,0:T(8,128)}, f32[64,128]{1,0:T(8,128)}) custom-call(f32[48,512]{1,0:T(8,128)} %add_add_fusion.refs_0_.refs_2_, bf16[48,32,512]{2,1,0:T(8,128)(2,1)} %constant_dynamic-update-slice_fusion.refs_1_.refs_5_, ...), custom_call_target="tpu_custom_call" | custom-call | flops 4000000000 | bytes 16000000 | tf_op jit(solution)/shard_map/pallas_call | solution.py:134
  145.0 10.7 %collective-permute-done.6.refs_3_.refs_4_ = bf16[48,32,512]{2,1,0:T(8,128)(2,1)} collective-permute-done((bf16[48,32,512]{2,1,0:T(8,128)(2,1)S(1)}, bf16[48,32,512]{2,1,0:T(8,128)(2,1)}, u32[]{:S(2)}, u32[]{:S(2)}) %collective-permute-start.6) | collective-permute-done | bytes 1572896 | tf_op jit(solution)/shard_map/ppermute | solution.py:315
  155.8 10.6 %last.1 = f32[32,8,128]{2,1,0:T(8,128)} custom-call(s32[10]{0:T(128)} %dynamic-slice_bitcast_fusion.refs_0_, f32[1]{0:T(128)} %dynamic_slice.8.refs_1_, f32[48,512]{1,0:T(8,128)} %add_add_fusion.refs_0_.refs_2_, bf16[48,32,512]{2,1,0:T(8,128)(2,1)} %collective-permute-done.6.refs_3_.refs_4_, bf16[48,32,512]{2,1,0:T(8,128)(2,1)} %collective-permute-done.6.refs_3_.refs_4_, ...), custom_call_target="tpu_custom_call" | custom-call | tf_op jit(solution)/shard_map/last/pallas_call | solution.py:254
  166.4 13.3 %all_to_all.5.refs_0_ = f32[32,8,128]{2,1,0:T(8,128)} all-to-all(f32[32,8,128]{2,1,0:T(8,128)} %last.1), channel_id=1, replica_groups=mesh['row'=4,'col'=8] {'row','col'}, dimensions={0} | all-to-all | bytes 262144 | tf_op jit(solution)/shard_map/all_to_all | solution.py:380
  179.7 1.8 finish.1
  (3 shorter events, 0.0 us)
Async XLA Ops:
  3.5 42.3 %copy-start.3 = (f32[48,512]{1,0:T(8,128)S(1)}, f32[48,512]{1,0:T(8,128)}, u32[]{:S(2)}) copy-start(f32[48,512]{1,0:T(8,128)} %get-tuple-element.12) | copy-start | bytes 294916
  3.5 37.6 %collective-permute-start.8 = (bf16[48,32,512]{2,1,0:T(8,128)(2,1)}, bf16[48,32,512]{2,1,0:T(8,128)(2,1)S(1)}, u32[]{:S(2)}, u32[]{:S(2)}) collective-permute-start(bf16[48,32,512]{2,1,0:T(8,128)(2,1)} %get-tuple-element.13.refs_1_.refs_7_.refs_9_.refs_15_.refs_3_), channel_id=1, source_target_pairs={{0,1},{1,0},{2,3},{3,2},{4,5},{5,4},{6,7},{7,6},{8,9},{9,8},{10,11... | collective-permute-start | bytes 4718600 | tf_op jit(solution)/shard_map/ppermute | solution.py:315
  6.5 36.5 %collective-permute-start.10 = (bf16[48,32,512]{2,1,0:T(8,128)(2,1)}, bf16[48,32,512]{2,1,0:T(8,128)(2,1)}, u32[]{:S(2)}, u32[]{:S(2)}) collective-permute-start(bf16[48,32,512]{2,1,0:T(8,128)(2,1)} %get-tuple-element.13.refs_1_.refs_7_.refs_9_.refs_15_.refs_3_), channel_id=1, source_target_pairs={{0,16},{1,17},{2,18},{3,19},{4,20},{5,21},{6,22},{7,23},{8,24},{9,... | collective-permute-start | bytes 4718600 | tf_op jit(solution)/shard_map/ppermute | solution.py:315
  8.0 111.9 %collective-permute-start.7 = (bf16[48,32,512]{2,1,0:T(8,128)(2,1)}, bf16[48,32,512]{2,1,0:T(8,128)(2,1)S(1)}, u32[]{:S(2)}, u32[]{:S(2)}) collective-permute-start(bf16[48,32,512]{2,1,0:T(8,128)(2,1)} %get-tuple-element.13.refs_1_.refs_7_.refs_9_.refs_15_.refs_3_), channel_id=1, source_target_pairs={{0,8},{1,9},{2,10},{3,11},{4,12},{5,13},{6,14},{7,15},{8,0},{9,1},... | collective-permute-start | bytes 4718600 | tf_op jit(solution)/shard_map/ppermute | solution.py:315
  41.1 70.8 %copy-start.1 = (bf16[48,32,512]{2,1,0:T(8,128)(2,1)}, bf16[48,32,512]{2,1,0:T(8,128)(2,1)S(1)}, u32[]{:S(2)}) copy-start(bf16[48,32,512]{2,1,0:T(8,128)(2,1)S(1)} %collective-permute-done.8.refs_3_.refs_11_) | copy-start | bytes 4718596
  41.1 35.1 %copy-start = (bf16[48,32,512]{2,1,0:T(8,128)(2,1)S(1)}, bf16[48,32,512]{2,1,0:T(8,128)(2,1)}, u32[]{:S(2)}) copy-start(bf16[48,32,512]{2,1,0:T(8,128)(2,1)} %get-tuple-element.13.refs_1_.refs_7_.refs_9_.refs_15_.refs_3_) | copy-start | bytes 4718596
  41.1 70.7 %collective-permute-start.13 = (bf16[24,32,512]{2,1,0:T(8,128)(2,1)S(1)}, bf16[24,32,512]{2,1,0:T(8,128)(2,1)S(1)}, u32[]{:S(2)}, u32[]{:S(2)}) collective-permute-start(bf16[24,32,512]{2,1,0:T(8,128)(2,1)S(1)} %slice.8), channel_id=1, source_target_pairs={{0,16},{1,17},{2,18},{3,19},{4,20},{5,21},{6,22},{7,23},{8,24},{9,... | collective-permute-start | bytes 2359304 | tf_op jit(solution)/shard_map/ppermute | solution.py:315
  44.2 69.1 %collective-permute-start.14 = (bf16[24,32,512]{2,1,0:T(8,128)(2,1)S(1)}, bf16[24,32,512]{2,1,0:T(8,128)(2,1)S(1)}, u32[]{:S(2)}, u32[]{:S(2)}) collective-permute-start(bf16[24,32,512]{2,1,0:T(8,128)(2,1)S(1)} %slice.9), channel_id=1, source_target_pairs={{0,1},{1,0},{2,3},{3,2},{4,5},{5,4},{6,7},{7,6},{8,9},{9,8},{10,11... | collective-permute-start | bytes 2359304 | tf_op jit(solution)/shard_map/ppermute | solution.py:315
  45.7 1.3 collective-permute-start
  47.1 17.5 %collective-permute-start.1 = (f32[48,512]{1,0:T(8,128)S(1)}, f32[48,512]{1,0:T(8,128)S(1)}, u32[]{:S(2)}, u32[]{:S(2)}) collective-permute-start(f32[48,512]{1,0:T(8,128)S(1)} %add.28), channel_id=1, source_target_pairs={{0,1},{1,0},{2,3},{3,2},{4,5},{5,4},{6,7},{7,6},{8,9},{9,8},{10,11... | collective-permute-start | bytes 294920 | tf_op jit(solution)/shard_map/ppermute | solution.py:315
  64.6 4.7 %collective-permute-start.2 = (f32[48,512]{1,0:T(8,128)S(1)}, f32[48,512]{1,0:T(8,128)S(1)}, u32[]{:S(2)}, u32[]{:S(2)}) collective-permute-start(f32[48,512]{1,0:T(8,128)S(1)} %add.29), channel_id=1, source_target_pairs={{0,16},{1,17},{2,18},{3,19},{4,20},{5,21},{6,22},{7,23},{8,24},{9,... | collective-permute-start | bytes 294920 | tf_op jit(solution)/shard_map/ppermute | solution.py:315
  69.3 53.0 %copy-start.4 = (f32[32]{0:T(128)S(1)}, f32[32]{0:T(128)}, u32[]{:S(2)}) copy-start(f32[32]{0:T(128)} %constant.23.clone) | copy-start | bytes 388
  69.3 6.8 %collective-permute-start.5 = (f32[48,512]{1,0:T(8,128)S(1)}, f32[48,512]{1,0:T(8,128)S(1)}, u32[]{:S(2)}, u32[]{:S(2)}) collective-permute-start(f32[48,512]{1,0:T(8,128)S(1)} %add.30), channel_id=1, source_target_pairs={{0,6},{1,7},{2,0},{3,1},{4,2},{5,3},{6,4},{7,5},{8,14},{9,15},{10,... | collective-permute-start | bytes 294920 | tf_op jit(solution)/shard_map/ppermute | solution.py:315
  73.0 38.9 %collective-permute-start.4 = (f32[48,512]{1,0:T(8,128)S(1)}, f32[48,512]{1,0:T(8,128)S(1)}, u32[]{:S(2)}, u32[]{:S(2)}) collective-permute-start(f32[48,512]{1,0:T(8,128)S(1)} %add.30), channel_id=1, source_target_pairs={{0,4},{1,5},{2,6},{3,7},{4,0},{5,1},{6,2},{7,3},{8,12},{9,13},{10,... | collective-permute-start | bytes 294920 | tf_op jit(solution)/shard_map/ppermute | solution.py:315
  76.2 48.7 %collective-permute-start.12 = (bf16[48,32,512]{2,1,0:T(8,128)(2,1)S(1)}, bf16[48,32,512]{2,1,0:T(8,128)(2,1)}, u32[]{:S(2)}, u32[]{:S(2)}) collective-permute-start(bf16[48,32,512]{2,1,0:T(8,128)(2,1)S(1)} %copy-done), channel_id=1, source_target_pairs={{0,2},{1,3},{2,4},{3,5},{4,6},{5,7},{6,0},{7,1},{8,10},{9,11},{10,... | collective-permute-start | bytes 4718600 | tf_op jit(solution)/shard_map/ppermute | solution.py:315
  111.9 13.0 %collective-permute-start.9 = (bf16[48,32,512]{2,1,0:T(8,128)(2,1)S(1)}, bf16[48,32,512]{2,1,0:T(8,128)(2,1)}, u32[]{:S(2)}, u32[]{:S(2)}) collective-permute-start(bf16[48,32,512]{2,1,0:T(8,128)(2,1)S(1)} %collective-permute-done.8.refs_3_.refs_11_), channel_id=1, source_target_pairs={{0,8},{1,9},{2,10},{3,11},{4,12},{5,13},{6,14},{7,15},{8,0},{9,1},... | collective-permute-start | bytes 4718600 | tf_op jit(solution)/shard_map/ppermute | solution.py:315
  111.9 13.0 %collective-permute-start.11 = (bf16[48,32,512]{2,1,0:T(8,128)(2,1)}, bf16[48,32,512]{2,1,0:T(8,128)(2,1)}, u32[]{:S(2)}, u32[]{:S(2)}) collective-permute-start(bf16[48,32,512]{2,1,0:T(8,128)(2,1)} %collective-permute-done.10.refs_5_.refs_13_), channel_id=1, source_target_pairs={{0,8},{1,9},{2,10},{3,11},{4,12},{5,13},{6,14},{7,15},{8,0},{9,1},... | collective-permute-start | bytes 4718600 | tf_op jit(solution)/shard_map/ppermute | solution.py:315
  113.3 6.6 %collective-permute-start.3 = (f32[48,512]{1,0:T(8,128)S(1)}, f32[48,512]{1,0:T(8,128)S(1)}, u32[]{:S(2)}, u32[]{:S(2)}) collective-permute-start(f32[48,512]{1,0:T(8,128)S(1)} %add.30), channel_id=1, source_target_pairs={{0,2},{1,3},{2,4},{3,5},{4,6},{5,7},{6,0},{7,1},{8,10},{9,11},{10,... | collective-permute-start | bytes 294920 | tf_op jit(solution)/shard_map/ppermute | solution.py:315
  119.9 17.3 %collective-permute-start.15 = (bf16[48,32,512]{2,1,0:T(8,128)(2,1)}, bf16[48,32,512]{2,1,0:T(8,128)(2,1)}, u32[]{:S(2)}, u32[]{:S(2)}) collective-permute-start(bf16[48,32,512]{2,1,0:T(8,128)(2,1)} %constant_dynamic-update-slice_fusion.refs_1_.refs_5_), channel_id=1, source_target_pairs={{0,8},{1,9},{2,10},{3,11},{4,12},{5,13},{6,14},{7,15},{8,0},{9,1},... | collective-permute-start | bytes 4718600 | tf_op jit(solution)/shard_map/ppermute | solution.py:315
  119.9 2.4 %copy-start.2 = (bf16[48,32,512]{2,1,0:T(8,128)(2,1)}, bf16[48,32,512]{2,1,0:T(8,128)(2,1)S(1)}, u32[]{:S(2)}) copy-start(bf16[48,32,512]{2,1,0:T(8,128)(2,1)S(1)} %collective-permute-done.7.refs_2_.refs_10_) | copy-start | bytes 4718596
  119.9 35.9 %collective-permute-start.6 = (bf16[48,32,512]{2,1,0:T(8,128)(2,1)S(1)}, bf16[48,32,512]{2,1,0:T(8,128)(2,1)}, u32[]{:S(2)}, u32[]{:S(2)}) collective-permute-start(bf16[48,32,512]{2,1,0:T(8,128)(2,1)S(1)} %copy-done), channel_id=1, source_target_pairs={{0,4},{1,5},{6,2},{7,3},{8,12},{9,13},{14,10},{15,11},{16,20},{17,... | collective-permute-start | bytes 4718600 | tf_op jit(solution)/shard_map/ppermute | solution.py:315
